TPU v7x, 128 devices: a whole 4x4x4 slice. The times are simulated.
128 devices in a mesh: expert: 8 (over x, core), tile: 16 (over z, y).
Axes of the slice: x: 4, y: 4, z: 4, core: 2. Of those that a mesh axis runs over, the one named last changes fastest.
Arguments:
- weight: bfloat16 [8, 2048, 8192], P('expert', None, 'tile'), may hold values from -6 to 6
- grad: bfloat16 [8, 2048, 8192], P('expert', None, 'tile'), may hold values from -24 to 24, as said below
- first_moment: float32 [8, 2048, 8192], P('expert', None, 'tile'), may hold values from -6 to 6
- second_moment: float32 [8, 2048, 8192], P('expert', None, 'tile'), may hold values from 0.25 to 4
- left_basis: bfloat16 [8, 1024, 2048], P('expert', None, 'tile'), may hold values from -1 to 1, as said below
- right_basis: bfloat16 [8, 1024, 8192], P('expert', None, 'tile'), may hold values from -1 to 1, as said below
Outputs:
- new_weight: bfloat16 [8, 2048, 8192], P('expert', None, 'tile')
- new_first: float32 [8, 2048, 8192], P('expert', None, 'tile')
- new_second: float32 [8, 2048, 8192], P('expert', None, 'tile')
Inputs may be any that keep to these rules, and one draw needn't show every extreme that they name: `grad`: scaled values. `left_basis`: every diagonal block is orthogonal before rounding to bfloat16. `right_basis`: every diagonal block is orthogonal before rounding to bfloat16.
All inputs are finite; a program needn't handle non-finite values.
Results may differ from a plain program's by a relative error of at most 0.0045.
Values may be sent and summed in bfloat16 or wider, within the bound.
No kernel may reach another device: no remote copies, remote signals or barrier semaphores. Data moves between devices by JAX's collectives and lax.ppermute only.
A program may use at most 128 MiB of HBM per device.

v0:
```python
import jax
import jax.numpy as jnp
from jax import lax
from jax.sharding import Mesh
from jax.sharding import PartitionSpec as P

TILE = ("tile_0", "tile_1")
EXPERT_TILE = ("expert_0", "expert_1", "tile_0", "tile_1")
EXPERT = ("expert_0", "expert_1")
beta_one = 0.9
beta_two = 0.95
epsilon = 1e-08
learn_rate = 0.25
decay_rate = 0.1


def one_axis_at_a_time(value, axes):
    for axis in axes:
        value = lax.psum(value, axis)
    return value


def swapped(value, axis, distance):
    mask = 2**distance
    pairs = [(source, source ^ mask) for source in range(lax.axis_size(axis))]
    return lax.ppermute(value, axis, pairs)


def doubling(items, position, send):
    other = send(items, 0)
    lower = position >> 0 & 1 == 0
    items = jnp.where(
        lower, jnp.concatenate((items, other), axis=2), jnp.concatenate((other, items), axis=2)
    )
    return items


def on_device(weight, grad, first_moment, second_moment, left_basis, right_basis):
    experts, rows, width = grad.shape
    block = right_basis.shape[1]
    group = block // width
    levels = group.bit_length() - 1
    position = lax.axis_index(TILE) % group
    left_count = rows // block
    local_total = jnp.sum(jnp.square(grad.astype(jnp.float32)))
    total = one_axis_at_a_time(local_total, EXPERT_TILE)
    count = experts * lax.axis_size(EXPERT) * rows * width * lax.axis_size(TILE)
    clip = 1.0 / jnp.maximum(1.0, jnp.sqrt(total / count))
    whole_left = lax.all_gather(left_basis, TILE, axis=2, tiled=True)
    left4 = whole_left.reshape(experts, block, left_count, block)
    grad4 = grad.reshape(experts, left_count, block, width)
    rotated_left = jnp.einsum("ekbi,ebkw->ebiw", left4, grad4, preferred_element_type=jnp.float32)
    rotated_left = rotated_left.reshape(experts, rows, width).astype(jnp.bfloat16)

    def send_rows(items, bit):
        return swapped(items, TILE, bit)

    left_block = doubling(rotated_left, position, send_rows)
    rotated = jnp.einsum(
        "edk,ekj->edj", left_block, right_basis, preferred_element_type=jnp.float32
    )
    clipped = clip * rotated
    new_first = beta_one * first_moment + (1.0 - beta_one) * clipped
    new_second = beta_two * second_moment + (1.0 - beta_two) * clipped * clipped
    update = (new_first / (jnp.sqrt(new_second) + epsilon)).astype(jnp.bfloat16)
    partial_term = jnp.einsum(
        "edj,ekj->edk", update, right_basis, preferred_element_type=jnp.float32
    )
    for bit in reversed(range(levels)):
        half = partial_term.shape[2] // 2
        first_half = partial_term[:, :, :half]
        second_half = partial_term[:, :, half:]
        upper = position >> bit & 1 == 1
        keeping = jnp.where(upper, second_half, first_half)
        sending = jnp.where(upper, first_half, second_half)
        partial_term = keeping + swapped(sending.astype(jnp.bfloat16), TILE, bit).astype(
            sending.dtype
        )
    back_right = partial_term.astype(jnp.bfloat16)
    back4 = back_right.reshape(experts, left_count, block, width)
    back = jnp.einsum("ekbi,ebiw->ebkw", left4, back4, preferred_element_type=jnp.float32).reshape(
        experts, rows, width
    )
    weight32 = weight.astype(jnp.float32)
    new_weight = (weight32 - learn_rate * (back + decay_rate * weight32)).astype(jnp.bfloat16)
    return (new_weight, new_first, new_second)


def solution(mesh):
    finer = Mesh(mesh.devices.reshape(4, 2, 4, 4), ("expert_0", "expert_1", "tile_0", "tile_1"))
    in_specs = (
        P(EXPERT, None, TILE),
        P(EXPERT, None, TILE),
        P(EXPERT, None, TILE),
        P(EXPERT, None, TILE),
        P(EXPERT, None, TILE),
        P(EXPERT, None, TILE),
    )
    out_specs = (P(EXPERT, None, TILE), P(EXPERT, None, TILE), P(EXPERT, None, TILE))
    return jax.shard_map(
        on_device, mesh=finer, in_specs=in_specs, out_specs=out_specs, check_vma=False
    )
```

profile of v0, /device:TPU:0, one launch (start us, length us, event | category | flops | bytes accessed | tf_op | source)
XLA Modules:
  0.0 212.0 jit_solution(10057856764942879282)
XLA Ops:
  7.2 0.0 copy-start
  7.2 0.0 all-gather.2.cloned.1.call-start
  7.2 0.7 all-gather.2.cloned.1.call-update
  7.9 0.0 copy-start.2
  7.9 61.7 %all-gather.2.cloned.1.call-done = bf16[1,1024,2048]{2,1,0:T(8,128)(2,1)} async-done(((bf16[1,1024,128]{2,1,0:T(8,128)(2,1)}), bf16[1,1024,2048]{2,1,0:T(8,128)(2,1)}) %all-gather.2.cloned.1.call-update) | async-done | bytes 4194320 | tf_op jit(solution)/shard_map/all_gather | solution.py:49
  69.6 6.4 %copy.12 = bf16[1,1024,2048]{1,2,0:T(8,128)(2,1)} copy(bf16[1,1024,2048]{2,1,0:T(8,128)(2,1)} %all-gather.2.cloned.1.call-done) | data formatting | bytes 8388608 | tf_op jit(solution)/shard_map/all_gather | solution.py:49
  76.0 0.0 copy-done.2
  76.0 5.8 %convolution_convert_fusion = bf16[2,1024,512]{2,1,0:T(8,128)(2,1)} fusion(bf16[1024,2,1024]{0,2,1:T(8,128)(2,1)} %bitcast.34, bf16[2,1024,512]{2,1,0:T(8,128)(2,1)S(1)} %bitcast.37), kind=kOutput, calls=%fused_computation.24 | convolution fusion | flops 2148532224 | bytes 8388608 | tf_op jit(solution)/shard_map/ekbi,ebkw->ebiw/dot_general | solution.py:52
  81.8 1.2 collective-permute-start
  83.0 1.7 multiply_reduce_fusion
  84.7 11.0 %psum.28 = f32[]{:T(128)} all-reduce(f32[]{:T(128)} %multiply_reduce_fusion), channel_id=1, replica_groups=mesh['expert_0'=4,'expert_1'=2,'tile_0'=4,'tile_1'=4] {'expert_0'}, use_global_device_ids=true, to_apply=%region_1.2 | all-reduce | flops 1 | bytes 8 | tf_op jit(solution)/shard_map/psum | solution.py:19
  95.7 3.1 %psum.29 = f32[]{:T(128)} all-reduce(f32[]{:T(128)} %psum.28), channel_id=1, replica_groups=mesh['expert_0'=4,'expert_1'=2,'tile_0'=4,'tile_1'=4] {'expert_1'}, use_global_device_ids=true, to_apply=%region_2.3 | all-reduce | flops 1 | bytes 8 | tf_op jit(solution)/shard_map/psum | solution.py:19
  98.8 9.8 %psum.30 = f32[]{:T(128)} all-reduce(f32[]{:T(128)} %psum.29), channel_id=1, replica_groups=mesh['expert_0'=4,'expert_1'=2,'tile_0'=4,'tile_1'=4] {'tile_0'}, use_global_device_ids=true, to_apply=%region_3.4 | all-reduce | flops 1 | bytes 8 | tf_op jit(solution)/shard_map/psum | solution.py:19
  108.6 24.2 %psum.31 = f32[]{:T(128)} all-reduce(f32[]{:T(128)} %psum.30), channel_id=1, replica_groups=mesh['expert_0'=4,'expert_1'=2,'tile_0'=4,'tile_1'=4] {'tile_1'}, use_global_device_ids=true, to_apply=%region_4.5 | all-reduce | flops 1 | bytes 8 | tf_op jit(solution)/shard_map/psum | solution.py:19
  133.5 0.0 collective-permute-done
  133.5 0.0 copy-done
  133.5 7.8 %fusion.4 = (f32[1,2048,512]{2,1,0:T(8,128)S(1)}, f32[1,2048,512]{2,1,0:T(8,128)S(1)}) fusion(f32[1,2048,512]{2,1,0:T(8,128)} %param.9, f32[]{:T(128)S(6)} %div.10, f32[1,2048,512]{2,1,0:T(8,128)} %param.8, bf16[1,1024,512]{2,1,0:T(8,128)(2,1)S(1)} %copy-done, bf16[2048,512]{1,0:T(8,128)(2,1)} %bitcast.4, bf16[2048,512]{1,0:T(8,128)(2,1)} %bitcast.2, pred[]{:T(512)S(6)} %eq.9), kind=kOutput, calls=%fused_computation.8 | convolution fusion | flops 2174746624 | bytes 22020100 | tf_op jit(solution)/shard_map/edk,ekj->edj/dot_general | solution.py:59
  141.4 0.0 copy-start.4
  141.4 0.0 copy-start.5
  141.4 2.8 %convolution_bitcast_fusion = f32[1,2048,1024]{2,1,0:T(8,128)S(1)} fusion(f32[1,2048,512]{2,1,0:T(8,128)S(1)} %get-tuple-element.4, f32[1,2048,512]{2,1,0:T(8,128)S(1)} %get-tuple-element.3, bf16[1,1024,512]{2,1,0:T(8,128)(2,1)S(1)} %copy-done), kind=kOutput, calls=%fused_computation.3 | convolution fusion | flops 2150629376 | bytes 17825792 | tf_op jit(solution)/shard_map/edj,ekj->edk/dot_general | solution.py:66
  144.2 0.0 copy-done.4
  144.2 0.5 copy-done.5
  144.7 0.4 select_convert_fusion
  145.1 0.0 copy-start.1
  145.1 0.3 collective-permute-start.1
  145.4 44.3 %collective-permute-done.1 = bf16[1,2048,512]{2,1,0:T(8,128)(2,1)S(1)} collective-permute-done((bf16[1,2048,512]{2,1,0:T(8,128)(2,1)S(1)}, bf16[1,2048,512]{2,1,0:T(8,128)(2,1)S(1)}, u32[]{:S(2)}, u32[]{:S(2)}) %collective-permute-start.1) | collective-permute-done | bytes 2097184 | tf_op jit(solution)/shard_map/ppermute | solution.py:26
  189.7 1.2 add_convert_fusion
  190.9 0.0 copy-done.1
  190.9 4.3 %convolution_bitcast_fusion.1 = f32[2,1024,512]{1,2,0:T(8,128)} fusion(bf16[2,1024,512]{2,1,0:T(8,128)(2,1)S(1)} %bitcast.36, bf16[1024,2,1024]{0,2,1:T(8,128)(2,1)S(1)} %bitcast.35), kind=kOutput, calls=%fused_computation.22 | convolution fusion | flops 2147483648 | bytes 10485760 | tf_op jit(solution)/shard_map/ekbi,ebiw->ebkw/dot_general | solution.py:81
  195.2 0.0 copy-start.3
  195.2 5.6 %copy.15 = f32[2,1024,512]{2,1,0:T(8,128)} copy(f32[2,1024,512]{1,2,0:T(8,128)} %convolution_bitcast_fusion.1) | data formatting | bytes 8388608 | tf_op jit(solution)/shard_map/ekbi,ebiw->ebkw/dot_general | solution.py:81
  200.8 0.0 copy-done.3
  200.8 4.3 %fusion.2 = bf16[1,2048,512]{2,1,0:T(8,128)(2,1)} fusion(bf16[1,2048,512]{2,1,0:T(8,128)(2,1)S(1)} %copy-done.3, f32[1,2048,512]{2,1,0:T(8,128)} %bitcast.33), kind=kLoop, calls=%fused_computation.6 | loop fusion | flops 6291456 | bytes 8388608 | tf_op jit(solution)/shard_map/convert_element_type | solution.py:85
Async XLA Ops:
  7.2 126.4 %copy-start = (bf16[1,1024,512]{2,1,0:T(8,128)(2,1)S(1)}, bf16[1,1024,512]{2,1,0:T(8,128)(2,1)}, u32[]{:S(2)}) copy-start(bf16[1,1024,512]{2,1,0:T(8,128)(2,1)} %param.11) | copy-start | bytes 3145732
  7.2 62.4 %all-gather.2.cloned.1.call-start = ((), (), s32[]{:S(2)}) async-start(), calls=%async_computation | async-start | bytes 4456448 | tf_op jit(solution)/shard_map/all_gather | solution.py:49
  7.9 68.1 %copy-start.2 = (bf16[1,2048,512]{2,1,0:T(8,128)(2,1)S(1)}, bf16[1,2048,512]{2,1,0:T(8,128)(2,1)}, u32[]{:S(2)}) copy-start(bf16[1,2048,512]{2,1,0:T(8,128)(2,1)} %param.7) | copy-start | bytes 6291460
  81.8 51.7 %collective-permute-start = (bf16[1,2048,512]{2,1,0:T(8,128)(2,1)}, bf16[1,2048,512]{2,1,0:T(8,128)(2,1)}, u32[]{:S(2)}, u32[]{:S(2)}) collective-permute-start(bf16[1,2048,512]{2,1,0:T(8,128)(2,1)} %bitcast.3), channel_id=1, source_target_pairs={{0,1},{1,0},{2,3},{3,2},{4,5},{5,4},{6,7},{7,6},{8,9},{9,8},{10,11... | collective-permute-start | bytes 6291464 | tf_op jit(solution)/shard_map/ppermute | solution.py:26
  141.4 2.8 %copy-start.4 = (f32[1,2048,512]{2,1,0:T(8,128)}, f32[1,2048,512]{2,1,0:T(8,128)S(1)}, u32[]{:S(2)}) copy-start(f32[1,2048,512]{2,1,0:T(8,128)S(1)} %get-tuple-element.3) | copy-start | bytes 12582916
  141.4 3.4 %copy-start.5 = (f32[1,2048,512]{2,1,0:T(8,128)}, f32[1,2048,512]{2,1,0:T(8,128)S(1)}, u32[]{:S(2)}) copy-start(f32[1,2048,512]{2,1,0:T(8,128)S(1)} %get-tuple-element.4) | copy-start | bytes 12582916
  145.1 45.8 %copy-start.1 = (bf16[1,1024,2048]{1,2,0:T(8,128)(2,1)S(1)}, bf16[1,1024,2048]{1,2,0:T(8,128)(2,1)}, u32[]{:S(2)}) copy-start(bf16[1,1024,2048]{1,2,0:T(8,128)(2,1)} %copy.12) | copy-start | bytes 12582916
  145.1 44.5 %collective-permute-start.1 = (bf16[1,2048,512]{2,1,0:T(8,128)(2,1)S(1)}, bf16[1,2048,512]{2,1,0:T(8,128)(2,1)S(1)}, u32[]{:S(2)}, u32[]{:S(2)}) collective-permute-start(bf16[1,2048,512]{2,1,0:T(8,128)(2,1)S(1)} %select_convert_fusion), channel_id=1, source_target_pairs={{0,1},{1,0},{2,3},{3,2},{4,5},{5,4},{6,7},{7,6},{8,9},{9,8},{10,11... | collective-permute-start | bytes 6291464 | tf_op jit(solution)/shard_map/ppermute | solution.py:26
  195.2 5.6 %copy-start.3 = (bf16[1,2048,512]{2,1,0:T(8,128)(2,1)S(1)}, bf16[1,2048,512]{2,1,0:T(8,128)(2,1)}, u32[]{:S(2)}) copy-start(bf16[1,2048,512]{2,1,0:T(8,128)(2,1)} %param.6) | copy-start | bytes 6291460
Sparse Core Ops, SparseCore 0:
  10.1 59.4 all-gather.1
where the time goes:
time: 212 us
  waiting for transfers between devices  107 us (50%)
  blocking collectives  48.1 us (23%)
  matrix products  20.8 us (10%)
  between operations  14.9 us (7%)
  local copies, waits for them, and re-layouts  12.5 us (6%)
  other arithmetic  7.61 us (4%)
    all_gather x1, waiting for transfers between devices, on_device(): whole_left = lax.all_gather(left_basis, TILE, axis=2, tiled=True)  61.7 us
    psum x4, blocking collectives, one_axis_at_a_time(): value = lax.psum(value, axis)  48.1 us
    ppermute x2, waiting for transfers between devices, swapped(): return lax.ppermute(value, axis, pairs)  44.3 us
    dot_general x1, matrix products, on_device(): jnp.einsum('edk,ekj->edj', left_block, right_basis, preferred_element_typ...  7.82 us
    all_gather x1, local copies, waits for them, and re-layouts, on_device(): whole_left = lax.all_gather(left_basis, TILE, axis=2, tiled=True)  6.4 us
    dot_general x1, matrix products, on_device(): jnp.einsum('ekbi,ebkw->ebiw', left4, grad4, preferred_element_type=jnp.fl...  5.83 us
    dot_general x1, local copies, waits for them, and re-layouts, on_device(): jnp.einsum('ekbi,ebiw->ebkw', left4, back4, preferred_element_type=jnp.fl...  5.56 us
    convert_element_type x1, other arithmetic, on_device(): (weight32 - learn_rate * (back + decay_rate * weight32)).astype(jnp.bfloa...  4.33 us
  transfers between devices with their start and end apart: 3, of which 2 were waited for; matrix products, arithmetic and copies ran while one was open for 1% of the time, Pallas kernels for 0%

commit v1 on v0

--- a/solution.py
+++ b/solution.py
@@ -46,7 +46,8 @@
     total = one_axis_at_a_time(local_total, EXPERT_TILE)
     count = experts * lax.axis_size(EXPERT) * rows * width * lax.axis_size(TILE)
     clip = 1.0 / jnp.maximum(1.0, jnp.sqrt(total / count))
-    whole_left = lax.all_gather(left_basis, TILE, axis=2, tiled=True)
+    outgoing = jnp.stack([left_basis] * lax.axis_size(TILE))
+    whole_left = jnp.concatenate(lax.all_to_all(outgoing, TILE, 0, 0), axis=2)
     left4 = whole_left.reshape(experts, block, left_count, block)
     grad4 = grad.reshape(experts, left_count, block, width)
     rotated_left = jnp.einsum("ekbi,ebkw->ebiw", left4, grad4, preferred_element_type=jnp.float32)

time: 212 us -> 184 us (0.87)
  waiting for transfers between devices: 107 us -> 43.3 us
  blocking collectives: 48.1 us -> 106 us
  between operations: 14.9 us -> 1.49 us
  matrix products: 20.8 us -> 15.9 us
  local copies, waits for them, and re-layouts: 12.5 us -> 7.84 us
    all_gather x1 -> x0, waiting for transfers between devices: 61.7 us -> none  [on_device(): whole_left = lax.all_gather(left_basis, TILE, axis=2, tiled=True)]
    all_to_all x0 -> x1, blocking collectives: none -> 58.9 us  [on_device(): whole_left = jnp.concatenate(lax.all_to_all(outgoing, TILE, 0, 0), axis=2)]
    all_gather x1 -> x0, local copies, waits for them, and re-layouts: 6.4 us -> none  [on_device(): whole_left = lax.all_gather(left_basis, TILE, axis=2, tiled=True)]
    dot_general x1, matrix products: 5.83 us -> 2.33 us  [on_device(): jnp.einsum('ekbi,ebkw->ebiw', left4, grad4, preferred_element_type=jnp.fl...]
  transfers between devices with their start and end apart: 3 -> 2, of which waited for: 2 -> 1; matrix products, arithmetic and copies ran while one was open for 1% -> 1% of each run, Pallas kernels for 0% -> 0%
where the time goes in v1:
time: 184 us
  blocking collectives  106 us (58%)
  waiting for transfers between devices  43.3 us (24%)
  matrix products  15.9 us (9%)
  local copies, waits for them, and re-layouts  7.84 us (4%)
  other arithmetic  7.61 us (4%)
  starting transfers between devices  2.1 us (1%)
    all_to_all x1, blocking collectives, on_device(): whole_left = jnp.concatenate(lax.all_to_all(outgoing, TILE, 0, 0), axis=2)  58.9 us
    psum x4, blocking collectives, one_axis_at_a_time(): value = lax.psum(value, axis)  46.8 us
    ppermute x2, waiting for transfers between devices, swapped(): return lax.ppermute(value, axis, pairs)  43.3 us
    dot_general x1, matrix products, on_device(): jnp.einsum('edk,ekj->edj', left_block, right_basis, preferred_element_typ...  6.46 us
    dot_general x1, local copies, waits for them, and re-layouts, on_device(): jnp.einsum('ekbi,ebiw->ebkw', left4, back4, preferred_element_type=jnp.fl...  5.56 us
    convert_element_type x1, other arithmetic, on_device(): (weight32 - learn_rate * (back + decay_rate * weight32)).astype(jnp.bfloa...  4.33 us
    dot_general x1, matrix products, on_device(): jnp.einsum('ekbi,ebiw->ebkw', left4, back4, preferred_element_type=jnp.fl...  4.3 us
  transfers between devices with their start and end apart: 2, of which 1 were waited for; matrix products, arithmetic and copies ran while one was open for 1% of the time, Pallas kernels for 0%

profile of v1, /device:TPU:0, one launch (start us, length us, event | category | flops | bytes accessed | tf_op | source)
XLA Modules:
  0.0 184.0 jit_solution(4391200850364214361)
XLA Ops:
  0.6 0.0 copy-start
  0.6 1.2 copy.16
  1.8 0.5 stack.2
  2.4 0.0 copy-start.3
  2.4 58.9 %all_to_all.5 = bf16[16,1,1024,128]{2,3,1,0:T(8,128)(2,1)S(1)} all-to-all(bf16[16,1,1024,128]{2,3,1,0:T(8,128)(2,1)S(1)} %stack.2), channel_id=1, replica_groups=mesh['expert_0'=4,'expert_1'=2,'tile_0'=4,'tile_1'=4] {'tile_0','tile_1'}, dimensions={0} | all-to-all | bytes 8388608 | tf_op jit(solution)/shard_map/all_to_all | solution.py:50
  61.3 0.0 copy-start.1
  61.3 0.0 copy-done.3
  61.3 2.3 %convolution_convert_fusion = bf16[2,1024,512]{2,1,0:T(8,128)(2,1)S(1)} fusion(bf16[1024,2,1024]{0,2,1:T(8,128)(2,1)S(1)} %bitcast.37, bf16[2,1024,512]{2,1,0:T(8,128)(2,1)S(1)} %bitcast.40), kind=kOutput, calls=%fused_computation.24 | convolution fusion | flops 2148532224 | bytes 8388608 | tf_op jit(solution)/shard_map/ekbi,ebkw->ebiw/dot_general | solution.py:53
  63.7 0.0 copy-done.1
  63.7 0.6 collective-permute-start
  64.3 1.7 multiply_reduce_fusion
  66.0 11.1 %psum.28 = f32[]{:T(128)} all-reduce(f32[]{:T(128)} %multiply_reduce_fusion), channel_id=1, replica_groups=mesh['expert_0'=4,'expert_1'=2,'tile_0'=4,'tile_1'=4] {'expert_0'}, use_global_device_ids=true, to_apply=%region_1.2 | all-reduce | flops 1 | bytes 8 | tf_op jit(solution)/shard_map/psum | solution.py:19
  77.1 3.1 %psum.29 = f32[]{:T(128)} all-reduce(f32[]{:T(128)} %psum.28), channel_id=1, replica_groups=mesh['expert_0'=4,'expert_1'=2,'tile_0'=4,'tile_1'=4] {'expert_1'}, use_global_device_ids=true, to_apply=%region_2.3 | all-reduce | flops 1 | bytes 8 | tf_op jit(solution)/shard_map/psum | solution.py:19
  80.2 9.2 %psum.30 = f32[]{:T(128)} all-reduce(f32[]{:T(128)} %psum.29), channel_id=1, replica_groups=mesh['expert_0'=4,'expert_1'=2,'tile_0'=4,'tile_1'=4] {'tile_0'}, use_global_device_ids=true, to_apply=%region_3.4 | all-reduce | flops 1 | bytes 8 | tf_op jit(solution)/shard_map/psum | solution.py:19
  89.3 23.5 %psum.31 = f32[]{:T(128)} all-reduce(f32[]{:T(128)} %psum.30), channel_id=1, replica_groups=mesh['expert_0'=4,'expert_1'=2,'tile_0'=4,'tile_1'=4] {'tile_1'}, use_global_device_ids=true, to_apply=%region_4.5 | all-reduce | flops 1 | bytes 8 | tf_op jit(solution)/shard_map/psum | solution.py:19
  113.5 0.0 collective-permute-done
  113.5 0.0 copy-done
  113.6 6.5 %fusion.4 = (f32[1,2048,512]{2,1,0:T(8,128)S(1)}, f32[1,2048,512]{2,1,0:T(8,128)S(1)}) fusion(f32[1,2048,512]{2,1,0:T(8,128)} %param.9, f32[]{:T(128)S(6)} %div.10, f32[1,2048,512]{2,1,0:T(8,128)} %param.8, bf16[1,1024,512]{2,1,0:T(8,128)(2,1)S(1)} %copy-done, bf16[2048,512]{1,0:T(8,128)(2,1)} %bitcast.6, bf16[2048,512]{1,0:T(8,128)(2,1)S(1)} %bitcast.43, ...), kind=kOutput, calls=%fused_computation.8 | convolution fusion | flops 2174746624 | bytes 22020100 | tf_op jit(solution)/shard_map/edk,ekj->edj/dot_general | solution.py:60
  120.0 0.0 copy-start.5
  120.0 0.0 copy-start.6
  120.0 2.8 %convolution_bitcast_fusion = f32[1,2048,1024]{2,1,0:T(8,128)S(1)} fusion(f32[1,2048,512]{2,1,0:T(8,128)S(1)} %get-tuple-element.4, f32[1,2048,512]{2,1,0:T(8,128)S(1)} %get-tuple-element.3, bf16[1,1024,512]{2,1,0:T(8,128)(2,1)S(1)} %copy-done), kind=kOutput, calls=%fused_computation.3 | convolution fusion | flops 2150629376 | bytes 17825792 | tf_op jit(solution)/shard_map/edj,ekj->edk/dot_general | solution.py:67
  122.9 0.0 copy-done.5
  122.9 0.5 copy-done.6
  123.4 0.4 select_convert_fusion
  123.8 0.0 copy-start.2
  123.8 1.5 collective-permute-start.1
  125.3 43.3 %collective-permute-done.1 = bf16[1,2048,512]{2,1,0:T(8,128)(2,1)S(1)} collective-permute-done((bf16[1,2048,512]{2,1,0:T(8,128)(2,1)S(1)}, bf16[1,2048,512]{2,1,0:T(8,128)(2,1)S(1)}, u32[]{:S(2)}, u32[]{:S(2)}) %collective-permute-start.1) | collective-permute-done | bytes 2097184 | tf_op jit(solution)/shard_map/ppermute | solution.py:26
  168.6 1.2 add_convert_fusion
  169.8 0.0 copy-done.2
  169.8 4.3 %convolution_bitcast_fusion.1 = f32[2,1024,512]{1,2,0:T(8,128)} fusion(bf16[2,1024,512]{2,1,0:T(8,128)(2,1)S(1)} %bitcast.39, bf16[1024,2,1024]{0,2,1:T(8,128)(2,1)S(1)} %bitcast.38), kind=kOutput, calls=%fused_computation.22 | convolution fusion | flops 2147483648 | bytes 10485760 | tf_op jit(solution)/shard_map/ekbi,ebiw->ebkw/dot_general | solution.py:82
  174.1 0.0 copy-start.4
  174.1 5.6 %copy.19 = f32[2,1024,512]{2,1,0:T(8,128)} copy(f32[2,1024,512]{1,2,0:T(8,128)} %convolution_bitcast_fusion.1) | data formatting | bytes 8388608 | tf_op jit(solution)/shard_map/ekbi,ebiw->ebkw/dot_general | solution.py:82
  179.7 0.0 copy-done.4
  179.7 4.3 %fusion.2 = bf16[1,2048,512]{2,1,0:T(8,128)(2,1)} fusion(bf16[1,2048,512]{2,1,0:T(8,128)(2,1)S(1)} %copy-done.4, f32[1,2048,512]{2,1,0:T(8,128)} %bitcast.36), kind=kLoop, calls=%fused_computation.6 | loop fusion | flops 6291456 | bytes 8388608 | tf_op jit(solution)/shard_map/convert_element_type | solution.py:86
Async XLA Ops:
  0.6 112.9 %copy-start = (bf16[1,1024,512]{2,1,0:T(8,128)(2,1)S(1)}, bf16[1,1024,512]{2,1,0:T(8,128)(2,1)}, u32[]{:S(2)}) copy-start(bf16[1,1024,512]{2,1,0:T(8,128)(2,1)} %param.11) | copy-start | bytes 3145732
  2.4 59.0 %copy-start.3 = (bf16[1,2048,512]{2,1,0:T(8,128)(2,1)S(1)}, bf16[1,2048,512]{2,1,0:T(8,128)(2,1)}, u32[]{:S(2)}) copy-start(bf16[1,2048,512]{2,1,0:T(8,128)(2,1)} %param.7) | copy-start | bytes 6291460
  61.3 2.3 %copy-start.1 = (bf16[16,1,1024,128]{2,3,1,0:T(8,128)(2,1)}, bf16[16,1,1024,128]{2,3,1,0:T(8,128)(2,1)S(1)}, u32[]{:S(2)}) copy-start(bf16[16,1,1024,128]{2,3,1,0:T(8,128)(2,1)S(1)} %all_to_all.5) | copy-start | bytes 12582916
  63.7 49.9 %collective-permute-start = (bf16[1,2048,512]{2,1,0:T(8,128)(2,1)S(1)}, bf16[1,2048,512]{2,1,0:T(8,128)(2,1)}, u32[]{:S(2)}, u32[]{:S(2)}) collective-permute-start(bf16[1,2048,512]{2,1,0:T(8,128)(2,1)S(1)} %bitcast.42), channel_id=1, source_target_pairs={{0,1},{1,0},{2,3},{3,2},{4,5},{5,4},{6,7},{7,6},{8,9},{9,8},{10,11... | collective-permute-start | bytes 6291464 | tf_op jit(solution)/shard_map/ppermute | solution.py:26
  120.0 2.8 %copy-start.5 = (f32[1,2048,512]{2,1,0:T(8,128)}, f32[1,2048,512]{2,1,0:T(8,128)S(1)}, u32[]{:S(2)}) copy-start(f32[1,2048,512]{2,1,0:T(8,128)S(1)} %get-tuple-element.3) | copy-start | bytes 12582916
  120.0 3.4 %copy-start.6 = (f32[1,2048,512]{2,1,0:T(8,128)}, f32[1,2048,512]{2,1,0:T(8,128)S(1)}, u32[]{:S(2)}) copy-start(f32[1,2048,512]{2,1,0:T(8,128)S(1)} %get-tuple-element.4) | copy-start | bytes 12582916
  123.8 46.0 %copy-start.2 = (bf16[16,1,1024,128]{2,3,1,0:T(8,128)(2,1)S(1)}, bf16[16,1,1024,128]{2,3,1,0:T(8,128)(2,1)}, u32[]{:S(2)}) copy-start(bf16[16,1,1024,128]{2,3,1,0:T(8,128)(2,1)} %copy-done.1) | copy-start | bytes 12582916
  123.8 44.8 %collective-permute-start.1 = (bf16[1,2048,512]{2,1,0:T(8,128)(2,1)S(1)}, bf16[1,2048,512]{2,1,0:T(8,128)(2,1)S(1)}, u32[]{:S(2)}, u32[]{:S(2)}) collective-permute-start(bf16[1,2048,512]{2,1,0:T(8,128)(2,1)S(1)} %select_convert_fusion), channel_id=1, source_target_pairs={{0,1},{1,0},{2,3},{3,2},{4,5},{5,4},{6,7},{7,6},{8,9},{9,8},{10,11... | collective-permute-start | bytes 6291464 | tf_op jit(solution)/shard_map/ppermute | solution.py:26
  174.1 5.6 %copy-start.4 = (bf16[1,2048,512]{2,1,0:T(8,128)(2,1)S(1)}, bf16[1,2048,512]{2,1,0:T(8,128)(2,1)}, u32[]{:S(2)}) copy-start(bf16[1,2048,512]{2,1,0:T(8,128)(2,1)} %param.6) | copy-start | bytes 6291460
